TPU v7x, 256 devices: a 2x2x32 block of a 4x8x32 slice. The times are simulated.
256 devices in a mesh: grp: 4 (over y, x), seq: 64 (over z, core).
Axes of the slice: x: 2, y: 2, z: 32, core: 2. Of those that a mesh axis runs over, the one named last changes fastest.
The devices are a block of a 4x8x32 slice.
Arguments:
- corpus: bfloat16 [65536, 3584], P(('grp', 'seq')), parts along dimension 0, may hold values from -6 to 6
- window_ends: int32 [512], P(('grp', 'seq')), parts along dimension 0, may hold values from 0 to 255
- norm_gain: float32 [3584], replicated, may hold values from 0.5 to 1.5
- routes: int32 [8192, 2], P(('grp', 'seq')), parts along dimension 0, may hold values from 0 to 63, all different within a row; in each aligned block of 32 rows (0 to 31, 32 to 63, ...) at most 2 rows name the same one
- in_blocks: int32 [64, 7], replicated, may hold values from 0 to 27, all different within a row
- out_blocks: int32 [64, 7], replicated, may hold values from 0 to 27, all different within a row
- enc_weight: bfloat16 [896, 131072], P(None, 'seq'), may hold values from -0.1875 to 0.1875
- enc_bias: float32 [131072], P('seq'), may hold values from -3 to 3
- latent_cutoffs: float32 [131072], P('seq'), may hold values from 0.2 to 1.2
- dec_weight: bfloat16 [131072, 896], P('seq'), may hold values from -0.125 to 0.125
- readout: float32 [131072], P('seq'), may hold values from -1.5 to 1.5
- dec_bias: float32 [3584], replicated, may hold values from -3 to 3
Outputs:
- reconstruction: bfloat16 [65536, 3584], P(('grp', 'seq')), parts along dimension 0
- attribution: bfloat16 [65536, 3584], P(('grp', 'seq')), parts along dimension 0
- feature_score: float32 [65536], P(('grp', 'seq')), parts along dimension 0
There are 4 independent parts, one for each index of `grp`. A program takes and returns all parts, laid end to end along the dimension named above; an argument that names none is the same for every part. Nothing has to cross between parts.
Inputs may be any that keep to these rules, and one draw needn't show every extreme that they name: `routes`: each segment names 2 different feature groups; within the 32 segments of one device no group is named more than 2 times. `in_blocks`: each row names 7 different blocks, and every block is named by some row. `out_blocks`: each row names 7 different blocks, and every block is named by some row.
All inputs are finite; a program needn't handle non-finite values.
Results may differ from a plain program's by a relative error of at most 0.012.
Values may be sent and summed in bfloat16 or wider, within the bound.
A program may use at most 128 MiB of HBM per device.

v0:
```python
import math

import jax
import jax.numpy as jnp
from jax import lax
from jax.sharding import PartitionSpec as P

BLK = 128
KEEP = 7
LEN = 128
SEG = 8


step_sharpness = 0.1
norm_eps = 1e-06


def from_behind(block, axis, distance):
    devices = range(lax.axis_size(axis))
    route = [(i - distance, i) for i in devices if i - distance in devices]
    return lax.ppermute(block, axis, route)


def side_by_side(arrays, axis, split_dim, concat_dim, along):
    widths = [math.prod(a.shape[along:]) for a in arrays]
    both = jnp.concatenate(
        [a.reshape(*a.shape[:along], w) for a, w in zip(arrays, widths)], axis=along
    )
    result = lax.all_to_all(both, axis, split_axis=split_dim, concat_axis=concat_dim, tiled=True)
    pieces = jnp.split(result, [sum(widths[:k]) for k in range(1, len(widths))], axis=along)
    return tuple(
        (b.reshape(*result.shape[:along], *a.shape[along:]) for a, b in zip(arrays, pieces))
    )


def normalize(rows, norm_gain):
    widened = rows.astype(jnp.float32)
    inverse_rms = lax.rsqrt(jnp.mean(widened * widened, axis=-1, keepdims=True) + norm_eps)
    return (widened * inverse_rms * norm_gain).astype(jnp.bfloat16)


def shards(
    corpus,
    window_ends,
    norm_gain,
    routes,
    in_blocks,
    out_blocks,
    enc_weight,
    enc_bias,
    latent_cutoffs,
    dec_weight,
    readout,
    dec_bias,
):
    devices = lax.axis_size("seq")
    model_width = corpus.shape[1]
    blocks_all = model_width // BLK
    below_rows = from_behind(corpus[-LEN:], "seq", 1)
    extended = jnp.concatenate([below_rows, corpus], axis=0)

    def take_one(end_offset):
        return lax.dynamic_slice_in_dim(extended, end_offset + 1, LEN, 0)

    windows = jax.vmap(take_one)(window_ends).reshape(-1, model_width)
    normal = normalize(windows, norm_gain)
    segments = normal.reshape(-1, SEG, model_width)
    seg_count = segments.shape[0]
    fanout = routes.shape[1]
    capacity = max(2, 2 * seg_count * fanout // devices)
    target = routes.reshape(-1)
    chosen_group = (target[:, None] == jnp.arange(devices, dtype=jnp.int32)[None, :]).astype(
        jnp.int32
    )
    before = jnp.cumsum(chosen_group, axis=0) - chosen_group
    rank_in_group = jnp.sum(before * chosen_group, axis=1)
    flat_slot = target * capacity + rank_in_group
    source_item = jnp.arange(target.shape[0], dtype=jnp.int32) // fanout
    slot_source = (
        jnp.full((devices * capacity,), seg_count, jnp.int32).at[flat_slot].set(source_item)
    )
    padded = jnp.concatenate([segments, jnp.zeros((1, SEG, model_width), segments.dtype)], axis=0)
    enc_blocks = enc_weight.reshape(KEEP, BLK, -1)
    block_grid = padded.reshape(seg_count + 1, SEG, blocks_all, BLK)
    outgoing = block_grid[
        slot_source.reshape(devices, capacity)[:, :, None], :, in_blocks[:, None, :]
    ]
    latent_input_level = (
        jnp.einsum(
            "ncqsb,qbf->ncsf",
            lax.all_to_all(outgoing, "seq", split_axis=0, concat_axis=0, tiled=True),
            enc_blocks,
            preferred_element_type=jnp.float32,
        )
        + enc_bias
    )
    exceeds_cutoff_indicator = jax.nn.sigmoid(
        (latent_input_level - latent_cutoffs) / step_sharpness
    )
    nonzero_latent_count = latent_input_level * exceeds_cutoff_indicator
    active_half = nonzero_latent_count.astype(jnp.bfloat16)
    rebuilt = jnp.einsum(
        "ncsf,fo->ncso", active_half, dec_weight, preferred_element_type=jnp.float32
    ).astype(jnp.bfloat16)
    score_part = jnp.sum(nonzero_latent_count * readout, axis=-1).astype(jnp.bfloat16)
    midpoint_gradient = (
        readout
        * (
            exceeds_cutoff_indicator
            + latent_input_level
            * exceeds_cutoff_indicator
            * (1.0 - exceeds_cutoff_indicator)
            / step_sharpness
        )
    ).astype(jnp.bfloat16)
    pulled = jnp.einsum(
        "ncsf,qbf->ncsqb", midpoint_gradient, enc_blocks, preferred_element_type=jnp.float32
    ).astype(jnp.bfloat16)
    returned = side_by_side((rebuilt, pulled, score_part), "seq", 0, 0, 3)
    recon_items = (
        returned[0]
        .reshape(devices * capacity, SEG, KEEP, BLK)[flat_slot]
        .reshape(seg_count, fanout, SEG, KEEP, BLK)
    )
    grad_items = (
        returned[1]
        .reshape(devices * capacity, SEG, KEEP, BLK)[flat_slot]
        .reshape(seg_count, fanout, SEG, KEEP, BLK)
    )
    block_ids = jnp.arange(blocks_all, dtype=jnp.int32)[None, None, :]
    place_out = (
        (out_blocks[target][:, :, None] == block_ids)
        .astype(jnp.bfloat16)
        .reshape(seg_count, fanout, KEEP, blocks_all)
    )
    place_in = (
        (in_blocks[target][:, :, None] == block_ids)
        .astype(jnp.bfloat16)
        .reshape(seg_count, fanout, KEEP, blocks_all)
    )
    recon_sum = jnp.einsum(
        "tkrqb,tkqj->trjb", recon_items, place_out, preferred_element_type=jnp.float32
    ).reshape(seg_count, SEG, model_width)
    grad_sum = jnp.einsum(
        "tkrqb,tkqj->trjb", grad_items, place_in, preferred_element_type=jnp.float32
    ).reshape(seg_count, SEG, model_width)
    score_items = returned[2].reshape(devices * capacity, SEG)[flat_slot]
    feature_score = jnp.sum(
        score_items.reshape(seg_count, fanout, SEG).astype(jnp.float32), axis=1
    ).reshape(-1)
    reconstruction = (recon_sum.reshape(-1, model_width) + dec_bias).astype(jnp.bfloat16)
    attribution = (normal.astype(jnp.float32) * grad_sum.reshape(-1, model_width)).astype(
        jnp.bfloat16
    )
    return (reconstruction, attribution, feature_score)


def solution(mesh):
    in_specs = (
        P(("grp", "seq"), None),
        P(("grp", "seq")),
        P(),
        P(("grp", "seq"), None),
        P(),
        P(),
        P(None, "seq"),
        P("seq"),
        P("seq"),
        P("seq", None),
        P("seq"),
        P(),
    )
    out_specs = (P(("grp", "seq"), None), P(("grp", "seq"), None), P(("grp", "seq")))
    return jax.shard_map(shards, mesh=mesh, in_specs=in_specs, out_specs=out_specs, check_vma=False)
```

profile of v0, /device:TPU:46, one launch (start us, length us, event | category | flops | bytes accessed | tf_op | source)
XLA Modules:
  0.0 652.1 jit_solution(5051480375739321806)
XLA Ops:
  0.6 1.2 slice.3
  1.9 2.8 collective-permute-start
  4.7 0.7 fusion.29
  5.3 0.8 copy.40
  6.3 0.7 fusion.31
  7.6 0.8 scatter_custom_fusion
  8.9 1.9 pad_maximum_fusion.1
  10.8 2.4 while.1
  10.8 1.2 bitcast_dynamic-update-slice_fusion.2
  12.0 1.2 bitcast_dynamic-update-slice_fusion.2
  13.2 1.9 multiply_reduce_fusion.1
  15.2 2.0 multiply_convert_fusion.2
  17.4 6.2 gather_fusion.1
  23.6 220.1 %all_to_all.10 = bf16[64,2,7,8,128]{4,3,2,1,0:T(8,128)(2,1)S(1)} all-to-all(bf16[64,2,7,8,128]{4,3,2,1,0:T(8,128)(2,1)} %bitcast.131), channel_id=1, replica_groups=mesh['grp'=4,'seq'=64] {'seq'}, dimensions={0} | all-to-all | bytes 3670016 | tf_op jit(solution)/shard_map/all_to_all | solution.py:91
  243.8 8.2 %multiply_reduce_fusion = (bf16[64,2,8]{2,1,0:T(2,128)(2,1)S(1)}, f32[64,2,8,2048,1]{3,2,4,1,0:T(8,128)}) fusion(f32[2048]{0:T(1024)S(1)} %copy-done.7, f32[2048]{0:T(1024)S(1)} %copy-done.8, f32[2048]{0:T(1024)S(1)} %copy-done.9, bf16[64,2,7,8,128]{4,3,2,1,0:T(8,128)(2,1)S(1)} %all_to_all.10, bf16[7,128,2048,1,1]{2,1,0,4,3:T(8,128)(2,1)S(1)} %bitcast.143), kind=kOutput, calls=%fused_computation.10 | convolution fusion | flops 3776969728 | bytes 13920256 | tf_op jit(solution)/shard_map/ncqsb,qbf->ncsf/dot_general | solution.py:89
  252.1 0.3 copy.46
  252.4 9.8 %convert_bitcast_fusion = bf16[64,2,8,896]{3,2,1,0:T(8,128)(2,1)S(1)} fusion(bf16[7,128,2048,1,1]{2,1,0,4,3:T(8,128)(2,1)} %bitcast.142, f32[2048]{0:T(1024)S(1)} %copy-done.8, f32[2048]{0:T(1024)S(1)} %copy-done.9, f32[64,2,8,2048,1]{3,2,4,1,0:T(8,128)} %get-tuple-element.42, f32[2048]{0:T(1024)S(1)} %copy-done.7), kind=kOutput, calls=%fused_computation.33 | convolution fusion | flops 3786276864 | bytes 13918208 | tf_op jit(solution)/shard_map/ncsf,qbf->ncsqb/dot_general | solution.py:116
  262.3 4.7 fusion.12
  266.9 2.1 pad_maximum_fusion
  269.0 7.6 %all-to-all-start.1 = ((bf16[64,2,8,1793]{3,2,1,0:T(8,128)(2,1)}), bf16[64,2,8,1793]{3,2,1,0:T(8,128)(2,1)}, u32[]{:S(2)}, u32[]{:S(2)}) async-start(bf16[64,2,8,1793]{3,2,1,0:T(8,128)(2,1)} %pad_maximum_fusion), calls=%async_computation.1 | async-start | bytes 7864320 | tf_op jit(solution)/shard_map/all_to_all | solution.py:29
  276.9 0.6 gather_fusion
  277.4 0.6 gather_fusion.3
  278.1 355.1 %all-to-all-done.1 = bf16[64,2,8,1793]{3,2,1,0:T(8,128)(2,1)} async-done(((bf16[64,2,8,1793]{3,2,1,0:T(8,128)(2,1)}), bf16[64,2,8,1793]{3,2,1,0:T(8,128)(2,1)}, u32[]{:S(2)}, u32[]{:S(2)}) %all-to-all-start.1) | async-done | bytes 3672096 | tf_op jit(solution)/shard_map/all_to_all | solution.py:29
  633.1 3.6 fusion.40
  636.7 0.7 gather_fusion.4
  637.5 2.2 gather_fusion.2
  639.7 1.2 slice_reduce_fusion
  640.9 0.6 gather_fusion.5
  641.6 0.7 reshape.189
  642.2 1.3 convolution_bitcast_fusion.1
  643.5 1.3 convolution_bitcast_fusion
  645.0 7.1 %fusion.5 = (bf16[256,3584]{1,0:T(8,128)(2,1)}, bf16[256,3584]{1,0:T(8,128)(2,1)}) fusion(f32[32,8,28,128]{3,2,1,0:T(8,128)S(1)} %convolution_bitcast_fusion, f32[3584]{0:T(1024)S(1)} %copy-done.1, f32[256]{0:T(256)S(1)} %get-tuple-element.37, bf16[2,128,3584]{2,1,0:T(8,128)(2,1)S(1)} %copy-done, f32[3584]{0:T(1024)S(1)} %copy-done.2, ...), kind=kLoop, calls=%fused_computation.20 | loop fusion | flops 8257536 | bytes 12874752 | tf_op jit(solution)/shard_map/convert_element_type | solution.py:152
  (49 shorter events, 2.1 us)
Async XLA Ops:
  1.9 7.0 %collective-permute-start = (bf16[128,3584]{1,0:T(8,128)(2,1)S(1)}, bf16[128,3584]{1,0:T(8,128)(2,1)}, u32[]{:S(2)}, u32[]{:S(2)}) collective-permute-start(bf16[128,3584]{1,0:T(8,128)(2,1)S(1)} %slice.3), channel_id=1, source_target_pairs={{0,1},{1,2},{2,3},{3,4},{4,5},{5,6},{6,7},{7,8},{8,9},{9,10},{10,1... | collective-permute-start | bytes 2752520 | tf_op jit(solution)/shard_map/ppermute | solution.py:21
  10.8 4.4 copy-start.1
  17.4 226.4 %copy-start.7 = (f32[2048]{0:T(1024)S(1)}, f32[2048]{0:T(1024)}, u32[]{:S(2)}) copy-start(f32[2048]{0:T(1024)} %param.22) | copy-start | bytes 24580
  17.4 226.4 %copy-start.8 = (f32[2048]{0:T(1024)S(1)}, f32[2048]{0:T(1024)}, u32[]{:S(2)}) copy-start(f32[2048]{0:T(1024)} %param.20) | copy-start | bytes 24580
  17.4 226.4 %copy-start.9 = (f32[2048]{0:T(1024)S(1)}, f32[2048]{0:T(1024)}, u32[]{:S(2)}) copy-start(f32[2048]{0:T(1024)} %param.19) | copy-start | bytes 24580
  23.6 220.2 %copy-start.5 = (bf16[896,2048]{1,0:T(8,128)(2,1)S(1)}, bf16[896,2048]{1,0:T(8,128)(2,1)}, u32[]{:S(2)}) copy-start(bf16[896,2048]{1,0:T(8,128)(2,1)} %param.18) | copy-start | bytes 11010052
  252.4 9.8 %copy-start.6 = (bf16[2048,896]{1,0:T(8,128)(2,1)S(1)}, bf16[2048,896]{1,0:T(8,128)(2,1)}, u32[]{:S(2)}) copy-start(bf16[2048,896]{1,0:T(8,128)(2,1)} %param.21) | copy-start | bytes 11010052
  252.4 9.8 %copy-start.10 = (f32[64,2,8,2048,1]{3,2,4,1,0:T(8,128)S(1)}, f32[64,2,8,2048,1]{3,2,4,1,0:T(8,128)}, u32[]{:S(2)}) copy-start(f32[64,2,8,2048,1]{3,2,4,1,0:T(8,128)} %get-tuple-element.42) | copy-start | bytes 25165828
  269.0 7.6 %copy-start.3 = (s32[64,7]{0,1:T(8,128)S(1)}, s32[64,7]{0,1:T(8,128)}, u32[]{:S(2)}) copy-start(s32[64,7]{0,1:T(8,128)} %param.16) | copy-start | bytes 5380
  269.0 7.7 %copy-start.4 = (s32[64,7]{0,1:T(8,128)S(1)}, s32[64,7]{0,1:T(8,128)}, u32[]{:S(2)}) copy-start(s32[64,7]{0,1:T(8,128)} %param.17) | copy-start | bytes 5380
  269.0 364.1 %all-to-all-start.1 = ((bf16[64,2,8,1793]{3,2,1,0:T(8,128)(2,1)}), bf16[64,2,8,1793]{3,2,1,0:T(8,128)(2,1)}, u32[]{:S(2)}, u32[]{:S(2)}) async-start(bf16[64,2,8,1793]{3,2,1,0:T(8,128)(2,1)} %pad_maximum_fusion), calls=%async_computation.1 | async-start | bytes 7864320 | tf_op jit(solution)/shard_map/all_to_all | solution.py:29
  643.5 1.5 copy-start
  643.5 1.5 copy-start.2
where the time goes:
time: 653 us; the launch traced here: 652 us
  waiting for transfers between devices  355 us (54%)
  blocking collectives  220 us (34%)
  matrix products  25.2 us (4%)
  local copies, waits for them, and re-layouts  23.4 us (4%)
  other arithmetic  17 us (3%)
  starting transfers between devices  10.4 us (2%)
    all_to_all x1, waiting for transfers between devices, side_by_side(): lax.all_to_all(both, axis, split_axis=split_dim, concat_axis=concat_dim,...  355 us
    all_to_all x1, blocking collectives, shards(): lax.all_to_all(outgoing, 'seq', split_axis=0, concat_axis=0, tiled=True)  220 us
  transfers between devices with their start and end apart: 2, of which 1 were waited for; matrix products, arithmetic and copies ran while one was open for 1% of the time, Pallas kernels for 0%

commit v1 on v0

v1 whole, which is shorter than its diff:
```python
import functools
import itertools

import jax
import jax.numpy as jnp
from jax import lax
from jax.experimental import pallas as pl
from jax.experimental.pallas import tpu as pltpu
from jax.sharding import PartitionSpec as P

BLK = 128
KEEP = 7
LEN = 128
SEG = 8
CAP = 2
CORES = 2
PIECES = 4

step_sharpness = 0.1
norm_eps = 1e-06

USUAL = (38, 36, 34, 31, 29, 27, 25, 24, 22, 20, 17, 15, 13, 11, 8, 5)


def most(hops):
    return tuple(CORES * CAP * (hops + 1 - t) for t in range(1, hops + 1))


def starts_of(limits):
    return tuple(itertools.accumulate((0,) + limits[:-1]))


def pieces_of(limits):
    size = -(-limits[0] // PIECES)
    pieces = [[(a, min(a + size, count)) for a in range(0, count, size)] for count in limits]
    firsts = starts_of(tuple(len(cut) for cut in pieces))
    return pieces, firsts, firsts[-1] + len(pieces[-1])


def ways(me, devices):
    return ((me + CORES) % devices, (me + devices - CORES) % devices)


def meet(others):
    barrier = pltpu.get_barrier_semaphore()
    for other in others:
        pl.semaphore_signal(
            barrier, inc=1, device_id={"seq": other}, device_id_type=pl.DeviceIdType.MESH
        )
    pl.semaphore_wait(barrier, len(others))


def to(other, src, dst, send_sem, recv_sem):
    return pltpu.make_async_remote_copy(
        src_ref=src,
        dst_ref=dst,
        send_sem=send_sem,
        recv_sem=recv_sem,
        device_id={"seq": other},
        device_id_type=pl.DeviceIdType.MESH,
    )


def carry_kernel(
    limits, devices, items, notes, x, heard, heard_near, lists, stage, known,
    s_data, r_data, s_note, r_note, s_near, r_near, s_last, r_last, read_sem,
):
    hops = len(limits)
    first = limits[0]
    pieces, firsts, _ = pieces_of(limits)
    slots = 4 * hops + 2
    me = lax.axis_index("seq")
    mate = me + 1 - 2 * (me % 2)
    onward = ways(me, devices)
    meet((*onward, mate))
    started = []

    def send(t, way, q, a, b):
        src = items.at[pl.ds(way * first + a, b - a)] if t == 1 else (
            lists[way][t - 2].at[pl.ds(a, b - a)]
        )
        copy = to(
            onward[way], src, lists[way][t - 1].at[pl.ds(a, b - a)],
            s_data.at[way, firsts[t - 1] + q], r_data.at[way, firsts[t - 1] + q],
        )
        copy.start()
        started.append(copy)
        return copy

    def send_note(t, way):
        src = notes.at[way] if t == 1 else heard.at[way, t - 2]
        copy = to(
            onward[way], src, heard.at[way, t - 1], s_note.at[way, t - 1], r_note.at[way, t - 1]
        )
        copy.start()
        started.append(copy)
        return copy

    note_copies = {}
    data_copies = {}
    for way in (0, 1):
        note_copies[1, way] = send_note(1, way)
    for q, (a, b) in enumerate(pieces[0]):
        for way in (0, 1):
            data_copies[1, way, q] = send(1, way, q, a, b)
    local = 2 * first
    near = to(
        mate, items.at[pl.ds(local + CAP, CAP)], x.at[pl.ds(slots + 4 * hops, CAP)],
        s_last.at[0], r_last.at[0],
    )
    near.start()
    near_note = to(mate, notes, heard_near.at[:, 0], s_last.at[1], r_last.at[1])
    near_note.start()
    mate_copies = [near, near_note]
    for j in range(CAP):
        x[4 * hops + j] = items[local + j]

    def hand_over(k, lo, hi):
        copy = to(
            mate, stage.at[pl.ds(4 * lo, 4 * (hi - lo))], x.at[pl.ds(slots + 4 * lo, 4 * (hi - lo))],
            s_near.at[k], r_near.at[k],
        )
        copy.start()
        mate_copies.append(copy)

    handed = 0
    batch = 4
    for t in range(1, hops + 1):
        reads = []
        for way in (0, 1):
            note_copies[t, way].wait_recv()
            if t < hops:
                note_copies[t + 1, way] = send_note(t + 1, way)
            reads.append(pltpu.make_async_copy(
                heard.at[way, t - 1], known.at[way, t - 1], read_sem.at[way, t - 1]
            ))
            reads[-1].start()
        following = pieces[t] if t < hops else []
        for q, _ in enumerate(pieces[t - 1]):
            for way in (0, 1):
                data_copies[t, way, q].wait_recv()
                if q < len(following):
                    data_copies[t + 1, way, q] = send(t + 1, way, q, *following[q])
        if t > 1 and (t - 1) % batch == 0:
            hand_over((t - 1) // batch - 1, handed, t - 1)
            handed = t - 1
        for read in reads:
            read.wait()
        for way in (0, 1):
            for j in range(CAP):
                slot = 4 * (t - 1) + CAP * way + j
                for who, out in ((me, x), (mate, stage)):
                    place = jnp.clip(known[way, t - 1, 0, j * devices + who], 0, limits[t - 1] - 1)
                    out[slot] = lists[way][t - 1][place]
    hand_over((hops - 1) // batch, handed, hops)
    relay = to(mate, heard, heard_near.at[:, pl.ds(1, hops)], s_last.at[2], r_last.at[2])
    relay.start()
    mate_copies.append(relay)
    for copy in mate_copies:
        copy.wait_recv()
    for copy in started + mate_copies:
        copy.wait_send()


def carry(limits, devices, items, notes, collective_id):
    hops = len(limits)
    slots = 4 * hops + 2
    piece_count = pieces_of(limits)[2]
    shape = items.shape[1:]
    batches = (hops - 1) // 4 + 1
    vmem = pl.BlockSpec(memory_space=pltpu.VMEM)
    smem = pl.BlockSpec(memory_space=pltpu.SMEM)
    dma = pltpu.SemaphoreType.DMA
    return pl.pallas_call(
        functools.partial(carry_kernel, limits, devices),
        out_shape=(
            jax.ShapeDtypeStruct((2 * slots, *shape), items.dtype),
            jax.ShapeDtypeStruct((2, hops, 1, notes.shape[-1]), jnp.int32),
            jax.ShapeDtypeStruct((2, hops + 1, 1, notes.shape[-1]), jnp.int32),
        ),
        in_specs=[vmem, vmem],
        out_specs=(vmem, vmem, vmem),
        scratch_shapes=[
            [[pltpu.VMEM((limit, *shape), items.dtype) for limit in limits] for _ in (0, 1)],
            pltpu.VMEM((4 * hops, *shape), items.dtype),
            pltpu.SMEM((2, hops, 1, notes.shape[-1]), jnp.int32),
            dma((2, piece_count)),
            dma((2, piece_count)),
            dma((2, hops)),
            dma((2, hops)),
            dma((batches,)),
            dma((batches,)),
            dma((3,)),
            dma((3,)),
            dma((2, hops)),
        ],
        compiler_params=pltpu.CompilerParams(
            collective_id=collective_id, has_side_effects=True, vmem_limit_bytes=60 << 20
        ),
        name=f"carry{collective_id}",
    )(items, notes)


def bring_kernel(
    limits, devices, y, score, heard, back, back_score, ring, ring_score, came_score, near, near_score,
    s_data, r_data, s_score, r_score, s_near, r_near,
):
    hops = len(limits)
    first = limits[0]
    starts = starts_of(limits)
    pieces, firsts, _ = pieces_of(limits)
    slots = 4 * hops + 2
    me = lax.axis_index("seq")
    mate = me + 1 - 2 * (me % 2)
    onward = ways(me, devices)
    meet((*onward, mate))
    batch = 4
    bounds = [(lo, min(lo + batch, hops)) for lo in range(0, hops, batch)]
    mate_copies = []
    spans = [(4 * lo, 4 * (hi - lo)) for lo, hi in reversed(bounds)] + [(4 * hops, CAP)]
    for k, (lo, size) in enumerate(spans):
        pair = []
        for m, (src, dst) in enumerate(((y, near), (score, near_score))):
            copy = to(
                mate, src.at[pl.ds(slots + lo, size)], dst.at[pl.ds(lo, size)],
                s_near.at[m, k], r_near.at[m, k],
            )
            copy.start()
            pair.append(copy)
        mate_copies.append(pair)
    for j in range(CAP):
        back[2 * first + j] = y[4 * hops + j]
    lane = lax.broadcasted_iota(jnp.int32, score.shape[1:], 1)

    started = []
    copies = {}

    def send(t, way, q, a, b):
        dst = back.at[pl.ds(way * first + a, b - a)] if t == 1 else (
            ring.at[way, pl.ds(starts[t - 2] + a, b - a)]
        )
        number = firsts[t - 1] + q
        copy = to(
            onward[1 - way], ring.at[way, pl.ds(starts[t - 1] + a, b - a)], dst,
            s_data.at[way, number], r_data.at[way, number],
        )
        copy.start()
        started.append(copy)
        copies[t, way, q] = copy

    def send_score(t, way):
        copy = to(
            onward[1 - way], ring_score.at[way, t - 1],
            back_score.at[way] if t == 1 else came_score.at[way, t - 2],
            s_score.at[way, t - 1], r_score.at[way, t - 1],
        )
        copy.start()
        started.append(copy)
        copies[t, way, None] = copy

    for t in range(hops, 0, -1):
        if (hops - t) % batch == 0:
            for copy in mate_copies[(hops - t) // batch]:
                copy.wait_recv()
        came = limits[t] if t < hops else 0
        mine = []
        for way in (0, 1):
            entries = []
            for who, own, own_score in ((me, y, score), (mate, near, near_score)):
                for j in range(CAP):
                    slot = 4 * (t - 1) + CAP * way + j
                    entries.append((
                        heard[way, t - 1, 0, j * devices + who], own, own_score, slot
                    ))
            mine.append(entries)
        for way in (0, 1):
            if t < hops:
                copies[t + 1, way, None].wait_recv()
                tile = came_score[way, t - 1]
            else:
                tile = jnp.zeros_like(lane, jnp.float32)
            for place, _, own_score, slot in mine[way]:
                tile = jnp.where(lane == place, own_score[slot], tile)
            ring_score[way, t - 1] = tile
        came_pieces = pieces[t] if t < hops else []
        for q, (a, b) in enumerate(pieces[t - 1]):
            for way in (0, 1):
                if q < len(came_pieces):
                    copies[t + 1, way, q].wait_recv()
                middle = max(a, min(b, came))
                base = starts[t - 1]
                entries = mine[way]

                def merge(k, old):
                    for place, own, _, slot in entries:
                        old = jnp.where(place == k, own[slot], old)
                    ring[way, base + k] = old

                def over(k, _):
                    merge(k, ring[way, base + k])
                    return 0

                def fresh(k, _):
                    merge(k, entries[0][1][entries[0][3]])
                    return 0

                if middle > a:
                    lax.fori_loop(a, middle, over, 0)
                if b > middle:
                    lax.fori_loop(middle, b, fresh, 0)
                send(t, way, q, a, b)
        for way in (0, 1):
            send_score(t, way)
    for copy in mate_copies[-1]:
        copy.wait_recv()
    tile = jnp.zeros_like(lane, jnp.float32)
    for j in range(CAP):
        back[2 * first + CAP + j] = near[4 * hops + j]
        tile = jnp.where(lane == j, score[4 * hops + j], tile)
        tile = jnp.where(lane == CAP + j, near_score[4 * hops + j], tile)
    back_score[2] = tile
    for (t, _, _), copy in copies.items():
        if t == 1:
            copy.wait_recv()
    for copy in started + [copy for pair in mate_copies for copy in pair]:
        copy.wait_send()


def bring(limits, devices, y, score, heard, collective_id):
    hops = len(limits)
    slots = 4 * hops + 2
    piece_count = pieces_of(limits)[2]
    shape = y.shape[1:]
    spans = (hops - 1) // 4 + 2
    total = 2 * limits[0] + 2 * CAP
    vmem = pl.BlockSpec(memory_space=pltpu.VMEM)
    smem = pl.BlockSpec(memory_space=pltpu.SMEM)
    dma = pltpu.SemaphoreType.DMA
    return pl.pallas_call(
        functools.partial(bring_kernel, limits, devices),
        out_shape=(
            jax.ShapeDtypeStruct((total, *shape), y.dtype),
            jax.ShapeDtypeStruct((3, *score.shape[1:]), score.dtype),
        ),
        in_specs=[vmem, vmem, smem],
        out_specs=(vmem, vmem),
        scratch_shapes=[
            pltpu.VMEM((2, sum(limits), *shape), y.dtype),
            pltpu.VMEM((2, hops, *score.shape[1:]), score.dtype),
            pltpu.VMEM((2, hops, *score.shape[1:]), score.dtype),
            pltpu.VMEM((slots, *shape), y.dtype),
            pltpu.VMEM((slots, *score.shape[1:]), score.dtype),
            dma((2, piece_count)),
            dma((2, piece_count)),
            dma((2, hops)),
            dma((2, hops)),
            dma((2, spans)),
            dma((2, spans)),
        ],
        compiler_params=pltpu.CompilerParams(
            collective_id=collective_id, has_side_effects=True, vmem_limit_bytes=60 << 20
        ),
        name=f"bring{collective_id}",
    )(y, score, heard)


def normalize(rows, norm_gain):
    widened = rows.astype(jnp.float32)
    inverse_rms = lax.rsqrt(jnp.mean(widened * widened, axis=-1, keepdims=True) + norm_eps)
    return (widened * inverse_rms * norm_gain).astype(jnp.bfloat16)


def plan(target, me, devices, limits):
    count = target.shape[0]
    chips = devices // CORES
    half = chips // 2
    index = jnp.arange(count, dtype=jnp.int32)
    dist = (target // CORES - me // CORES + chips) % chips
    away = dist > 0
    order = dist * count + index
    rank = jnp.sum(((order[None, :] < order[:, None]) & away[None, :]).astype(jnp.int32), axis=1)
    total = jnp.sum(away.astype(jnp.int32))
    least = jnp.sum((away & (dist < half)).astype(jnp.int32))
    upmost = jnp.sum((away & (dist <= half)).astype(jnp.int32))
    cut = jnp.clip((total + 1 - me % CORES) // 2, least, upmost)
    up = rank < cut
    place = jnp.where(up, cut - 1 - rank, rank - cut)
    hop = jnp.where(up, dist, chips - dist)
    way = jnp.where(away, jnp.where(up, 0, 1), 2)
    room = jnp.zeros_like(place)
    for t, limit in enumerate(limits, 1):
        room = jnp.where(hop == t, limit, room)
    fits = place < room
    same = (target[None, :] == target[:, None]) & (index[None, :] < index[:, None])
    pair = jnp.sum(same.astype(jnp.int32), axis=1)
    first = limits[0]
    at_home = 2 * first + jnp.where(target == me, 0, CAP) + pair
    entry = jnp.where(away, way * first + place, at_home)
    lines = jnp.arange(2 * first + 2 * CAP, dtype=jnp.int32)
    held = (lines[:, None] == entry[None, :]) & (fits | ~away)[None, :]
    item_of = jnp.sum(jnp.where(held, index[None, :], 0), axis=1)
    lane = pair * devices + target
    lanes = jnp.arange(CAP * devices, dtype=jnp.int32)
    value = jnp.where(fits, place + 1, -1)
    notes = jnp.stack([
        jnp.sum(
            jnp.where((lanes[:, None] == lane[None, :]) & (way == w)[None, :], value[None, :], 0),
            axis=1,
        )
        for w in (0, 1)
    ]) - 1
    return entry, item_of, notes.reshape(2, 1, -1)


def shards(
    corpus,
    window_ends,
    norm_gain,
    routes,
    in_blocks,
    out_blocks,
    enc_weight,
    enc_bias,
    latent_cutoffs,
    dec_weight,
    readout,
    dec_bias,
    usual=USUAL,
):
    devices = lax.axis_size("seq")
    me = lax.axis_index("seq")
    hops = devices // CORES // 2
    model_width = corpus.shape[1]
    blocks_all = model_width // BLK
    below_rows = lax.ppermute(
        corpus[-LEN:], "seq", [(i, i + 1) for i in range(devices - 1)]
    )
    extended = jnp.concatenate([below_rows, corpus], axis=0)

    def take_one(end_offset):
        return lax.dynamic_slice_in_dim(extended, end_offset + 1, LEN, 0)

    windows = jax.vmap(take_one)(window_ends).reshape(-1, model_width)
    normal = normalize(windows, norm_gain)
    segments = normal.reshape(-1, SEG, model_width)
    seg_count = segments.shape[0]
    fanout = routes.shape[1]
    target = routes.reshape(-1)
    block_grid = segments.reshape(seg_count, SEG, blocks_all, BLK)
    enc_blocks = enc_weight.reshape(KEEP, BLK, -1)

    def out(limits, collective_id):
        entry, item_of, notes = plan(target, me, devices, limits)
        outgoing = block_grid[(item_of // fanout)[:, None], :, in_blocks[target[item_of]]]
        x, heard, heard_near = carry(limits, devices, outgoing, notes, collective_id)
        return x, heard, entry, notes, heard_near

    def home(limits, collective_id, y, score, heard, entry):
        back, back_score = bring(limits, devices, y, score, heard, collective_id)
        first = limits[0]
        column = jnp.where(
            entry < first, entry,
            jnp.where(entry < 2 * first, BLK - first + entry, 2 * BLK - 2 * first + entry),
        )
        columns = jnp.arange(3 * BLK, dtype=jnp.int32).reshape(3, 1, BLK)
        picked_score = jnp.sum(
            jnp.where(columns[None] == column[:, None, None, None], back_score[None], 0.0),
            axis=(1, 3),
        )
        return back[entry], picked_score

    limits = most(hops)
    x, heard, entry, notes, heard_near = out(usual, 0)
    crowded = jnp.minimum(
        jnp.min(heard), jnp.minimum(jnp.min(heard_near), jnp.min(notes))
    ) < -1
    x, heard, entry = lax.cond(
        crowded, lambda: out(limits, 2)[:3], lambda: (x, heard, entry)
    )
    level = (
        jnp.einsum("nqsb,qbf->nsf", x, enc_blocks, preferred_element_type=jnp.float32)
        + enc_bias
    )
    firing = jax.nn.sigmoid((level - latent_cutoffs) / step_sharpness)
    active = level * firing
    active_half = active.astype(jnp.bfloat16)
    decoded = jnp.einsum(
        "nsf,fo->nso", active_half, dec_weight, preferred_element_type=jnp.float32
    ).astype(jnp.bfloat16)
    score = jnp.sum(active * readout, axis=-1).astype(jnp.bfloat16).astype(jnp.float32)
    slope = (
        readout * (firing + level * firing * (1.0 - firing) / step_sharpness)
    ).astype(jnp.bfloat16)
    pulled = jnp.einsum(
        "nsf,qbf->nqsb", slope, enc_blocks, preferred_element_type=jnp.float32
    ).astype(jnp.bfloat16)
    decoded = decoded.reshape(-1, SEG, KEEP, BLK).transpose(0, 2, 1, 3)
    y = jnp.concatenate([decoded, pulled], axis=1)
    score = jnp.broadcast_to(score[:, :, None], (*score.shape, BLK))
    picked, picked_score = lax.cond(
        crowded,
        lambda: home(limits, 3, y, score, heard, entry),
        lambda: home(usual, 1, y, score, heard, entry),
    )
    recon_items = picked[:, :KEEP].reshape(seg_count, fanout, KEEP, SEG, BLK)
    grad_items = picked[:, KEEP:].reshape(seg_count, fanout, KEEP, SEG, BLK)
    block_ids = jnp.arange(blocks_all, dtype=jnp.int32)[None, None, :]

    def placed(blocks, values):
        where = (
            (blocks[target][:, :, None] == block_ids)
            .astype(jnp.bfloat16)
            .reshape(seg_count, fanout, KEEP, blocks_all)
        )
        return jnp.einsum(
            "tkqrb,tkqj->trjb", values, where, preferred_element_type=jnp.float32
        ).reshape(-1, model_width)

    recon_sum = placed(out_blocks, recon_items)
    grad_sum = placed(in_blocks, grad_items)
    feature_score = jnp.sum(
        picked_score.reshape(seg_count, fanout, SEG), axis=1
    ).reshape(-1)
    reconstruction = (recon_sum + dec_bias).astype(jnp.bfloat16)
    attribution = (normal.astype(jnp.float32) * grad_sum).astype(jnp.bfloat16)
    return reconstruction, attribution, feature_score


def solution(mesh):
    in_specs = (
        P(("grp", "seq"), None),
        P(("grp", "seq")),
        P(),
        P(("grp", "seq"), None),
        P(),
        P(),
        P(None, "seq"),
        P("seq"),
        P("seq"),
        P("seq", None),
        P("seq"),
        P(),
    )
    out_specs = (P(("grp", "seq"), None), P(("grp", "seq"), None), P(("grp", "seq")))
    return jax.shard_map(shards, mesh=mesh, in_specs=in_specs, out_specs=out_specs, check_vma=False)
```

time: 653 us -> 477 us (0.73)
  Pallas kernels: 0 us -> 384 us
  waiting for transfers between devices: 355 us -> 0.01 us
  blocking collectives: 220 us -> 0 us
  loops' own time: 0.02 us -> 15.1 us
  starting transfers between devices: 10.4 us -> 2.77 us
    pallas_call x0 -> x2, Pallas kernels: none -> 384 us  [the longest x1 237 us: bring(): pl.pallas_call(functools.partial(bring_kernel, limits, devices), out_shap...]
    all_to_all x1 -> x0, waiting for transfers between devices: 355 us -> none  [side_by_side(): lax.all_to_all(both, axis, split_axis=split_dim, concat_axis=concat_dim,...]
    all_to_all x1 -> x0, blocking collectives: 220 us -> none  [shards(): lax.all_to_all(outgoing, 'seq', split_axis=0, concat_axis=0, tiled=True)]
    another operation x0 -> x2, loops' own time: none -> 15 us  [the longest x1 9.14 us: shards(): lax.cond(crowded, lambda: out(limits, 2)[:3], lambda: (x, heard, entry))]
    all_to_all x1 -> x0, starting transfers between devices: 7.63 us -> none  [side_by_side(): lax.all_to_all(both, axis, split_axis=split_dim, concat_axis=concat_dim,...]
  transfers between devices with their start and end apart: 2 -> 1, of which waited for: 1 -> 0; matrix products, arithmetic and copies ran while one was open for 1% -> 2% of each run, Pallas kernels for 0% -> 0%
where the time goes in v1:
time: 477 us; the launch traced here: 471 us
  Pallas kernels  384 us (81%)
  matrix products  22.9 us (5%)
  other arithmetic  21.1 us (4%)
  local copies, waits for them, and re-layouts  19.9 us (4%)
  loops' own time  15.1 us (3%)
  between operations  5.17 us (1%)
    pallas_call x1, Pallas kernels, bring(): pl.pallas_call(functools.partial(bring_kernel, limits, devices), out_shap...  237 us
    pallas_call x1, Pallas kernels, carry(): pl.pallas_call(functools.partial(carry_kernel, limits, devices), out_shap...  147 us
  transfers between devices with their start and end apart: 1, of which 0 were waited for; matrix products, arithmetic and copies ran while one was open for 2% of the time, Pallas kernels for 0%

profile of v1, /device:TPU:46, one launch (start us, length us, event | category | flops | bytes accessed | tf_op | source)
XLA Modules:
  0.0 470.5 jit_solution(4810505076510858368)
XLA Ops:
  0.6 1.2 slice.9
  1.9 2.8 collective-permute-start
  4.6 1.4 convert_reduce_fusion.5
  6.7 0.8 copy.40
  9.4 1.2 gather_fusion.6
  10.7 0.8 copy.44
  11.5 0.6 gather_fusion.7
  12.3 0.7 fusion.59
  13.7 0.8 copy.41
  15.2 1.2 fusion.70
  16.4 1.9 pad_maximum_fusion.1
  18.3 2.4 while.1
  18.3 1.2 bitcast_dynamic-update-slice_fusion.2
  19.5 1.2 bitcast_dynamic-update-slice_fusion.2
  20.7 1.9 multiply_reduce_fusion.1
  22.8 2.1 multiply_convert_fusion.2
  24.8 6.5 %gather_fusion.8 = bf16[560,8,128]{2,1,0:T(8,128)(2,1)} fusion(bf16[32,8,28,128]{3,1,2,0:T(8,128)(2,1)S(1)} %multiply_convert_fusion.2, s32[560]{0:T(1024)S(1)} %reshape.711), kind=kCustom, calls=%fused_computation.8 | custom fusion | bytes 2298240 | tf_op jit(solution)/shard_map/gather | solution.py:454
  31.3 146.6 %carry0.1 = (bf16[132,7,8,128]{3,2,1,0:T(8,128)(2,1)}, s32[2,16,1,128]{3,2,1,0:T(1,128)S(1)}, s32[2,17,1,128]{3,2,1,0:T(1,128)}) custom-call(bf16[80,7,8,128]{3,2,1,0:T(8,128)(2,1)} %bitcast.146, s32[2,1,128]{2,1,0:T(1,128)} %get-tuple-element.231.notes), custom_call_target="tpu_custom_call" | custom-call | tf_op jit(solution)/shard_map/carry0/pallas_call | solution.py:174
  177.9 1.4 reduce_min.28
  179.3 0.7 reduce_min.27
  182.0 9.6 %conditional.2 = (bf16[132,7,8,128]{3,2,1,0:T(8,128)(2,1)}, s32[2,16,1,128]{3,2,1,0:T(1,128)S(1)}, s32[64]{0:T(128)}) conditional(s32[]{:T(128)} %convert_element_type.117, (pred[64]{0:T(512)(128)(4,1)S(1)}, s32[64]{0:T(128)S(1)}, s32[64]{0:T(128)S(1)}, pred[64]{0:T(512)(128)(4,1)S(1)}, s32[64]{0:T(128)S(1)}, /*index=5*/s32[]{:T(128)}, ...), branch_computations={%region_12.13_spmd, %region_13.22_spmd} | conditional | flops 145584 | bytes 3845029 | solution.py:477
  191.7 8.8 %multiply_reduce_fusion = (bf16[132,8]{1,0:T(8,128)(2,1)S(1)}, f32[132,8,2048,1]{2,1,3,0:T(8,128)S(1)}) fusion(f32[2048]{0:T(1024)S(1)} %copy-done.10, f32[2048]{0:T(1024)S(1)} %copy-done.11, f32[2048]{0:T(1024)S(1)} %copy-done.12, bf16[132,7,8,128]{3,2,1,0:T(8,128)(2,1)} %get-tuple-element.167, bf16[7,128,2048,1]{2,1,0,3:T(8,128)(2,1)} %bitcast.165), kind=kOutput, calls=%fused_computation.105 | convolution fusion | flops 3895000064 | bytes 14239808 | tf_op jit(solution)/shard_map/nqsb,qbf->nsf/dot_general | solution.py:481
  200.5 6.6 %convert_bitcast_fusion = bf16[132,7,8,128]{3,2,1,0:T(8,128)(2,1)S(1)} fusion(bf16[7,128,2048,1]{2,1,0,3:T(8,128)(2,1)S(1)} %bitcast.166, f32[2048]{0:T(1024)S(1)} %copy-done.11, f32[2048]{0:T(1024)S(1)} %copy-done.12, f32[132,8,2048,1]{2,1,3,0:T(8,128)S(1)} %get-tuple-element.258, f32[2048]{0:T(1024)S(1)} %copy-done.10), kind=kOutput, calls=%fused_computation.126 | convolution fusion | flops 3904598016 | bytes 14237696 | tf_op jit(solution)/shard_map/nsf,qbf->nqsb/dot_general | solution.py:494
  207.1 5.0 %convert_bitcast_fusion.1 = bf16[132,7,8,128]{3,2,1,0:T(8,128)(2,1)S(1)} fusion(bf16[2048,896]{1,0:T(8,128)(2,1)S(1)} %copy-done.9, f32[132,8,2048,1]{2,1,3,0:T(8,128)S(1)} %get-tuple-element.258, f32[2048]{0:T(1024)S(1)} %copy-done.11, f32[2048]{0:T(1024)S(1)} %copy-done.12), kind=kOutput, calls=%fused_computation.127 | convolution fusion | flops 3893784576 | bytes 14229504 | tf_op jit(solution)/shard_map/nsf,fo->nso/dot_general | solution.py:487
  212.6 247.5 %conditional.3 = (bf16[64,14,8,128]{3,2,1,0:T(8,128)(2,1)S(1)}, f32[256]{0:T(256)S(1)}) conditional(s32[]{:T(128)} %convert_element_type.117, (f32[132,8,1]{1,0,2:T(8,128)S(1)}, bf16[132,14,8,128]{3,2,1,0:T(8,128)(2,1)S(1)}, s32[2,16,1,128]{3,2,1,0:T(1,128)S(1)}, s32[64]{0:T(128)}) %tuple.31, (f32[132,8,1]{1,0,2:T(8,128)S(1)}, ...), branch_computations={%region_23.26_spmd, %region_26.29_spmd} | conditional | flops 419904 | bytes 4341424 | solution.py:500
  212.6 1.0 broadcast_in_dim.248.score
  213.6 237.0 %bring1.1 = (bf16[80,14,8,128]{3,2,1,0:T(8,128)(2,1)}, f32[3,8,128]{2,1,0:T(8,128)}) custom-call(bf16[132,14,8,128]{3,2,1,0:T(8,128)(2,1)S(1)} %get-tuple-element.141.y, f32[132,8,128]{2,1,0:T(8,128)} %broadcast_in_dim.248.score, s32[2,16,1,128]{3,2,1,0:T(1,128)S(1)} %get-tuple-element.143.heard), custom_call_target="tpu_custom_call" | custom-call | tf_op jit(solution)/shard_map/cond/branch_0_fun/bring1/pallas_call | solution.py:339
  451.2 2.6 gather_fusion
  460.3 1.3 convolution_bitcast_fusion
  461.6 4.2 fusion.24
  465.7 1.3 convolution_bitcast_fusion.1
  467.0 3.3 fusion.25
  (69 shorter events, 4.6 us)
Async XLA Ops:
  1.9 14.5 %collective-permute-start = (bf16[128,3584]{1,0:T(8,128)(2,1)S(1)}, bf16[128,3584]{1,0:T(8,128)(2,1)}, u32[]{:S(2)}, u32[]{:S(2)}) collective-permute-start(bf16[128,3584]{1,0:T(8,128)(2,1)S(1)} %slice.9), channel_id=1, source_target_pairs={{0,1},{1,2},{2,3},{3,4},{4,5},{5,6},{6,7},{7,8},{8,9},{9,10},{10,1... | collective-permute-start | bytes 2752520 | tf_op jit(solution)/shard_map/ppermute | solution.py:435
  18.3 4.4 copy-start.1
  22.7 159.2 %copy-start.3 = (s32[64,7]{0,1:T(8,128)S(1)}, s32[64,7]{0,1:T(8,128)}, u32[]{:S(2)}) copy-start(s32[64,7]{0,1:T(8,128)} %param.20) | copy-start | bytes 5380
  22.7 159.2 %copy-start.6 = (s32[32,2]{0,1:T(2,128)S(1)}, s32[32,2]{0,1:T(2,128)}, u32[]{:S(2)}) copy-start(s32[32,2]{0,1:T(2,128)} %param.19) | copy-start | bytes 772
  182.0 9.7 %copy-start.10 = (f32[2048]{0:T(1024)S(1)}, f32[2048]{0:T(1024)}, u32[]{:S(2)}) copy-start(f32[2048]{0:T(1024)} %param.26) | copy-start | bytes 24580
  182.0 9.7 %copy-start.11 = (f32[2048]{0:T(1024)S(1)}, f32[2048]{0:T(1024)}, u32[]{:S(2)}) copy-start(f32[2048]{0:T(1024)} %param.24) | copy-start | bytes 24580
  182.0 9.7 %copy-start.12 = (f32[2048]{0:T(1024)S(1)}, f32[2048]{0:T(1024)}, u32[]{:S(2)}) copy-start(f32[2048]{0:T(1024)} %param.23) | copy-start | bytes 24580
  191.7 8.8 %copy-start.8 = (bf16[896,2048]{1,0:T(8,128)(2,1)S(1)}, bf16[896,2048]{1,0:T(8,128)(2,1)}, u32[]{:S(2)}) copy-start(bf16[896,2048]{1,0:T(8,128)(2,1)} %param.22) | copy-start | bytes 11010052
  200.5 6.6 %copy-start.9 = (bf16[2048,896]{1,0:T(8,128)(2,1)S(1)}, bf16[2048,896]{1,0:T(8,128)(2,1)}, u32[]{:S(2)}) copy-start(bf16[2048,896]{1,0:T(8,128)(2,1)} %param.25) | copy-start | bytes 11010052
  450.6 3.3 copy-start.4
  460.1 1.4 copy-start.7
  460.1 1.5 copy-start
  465.7 1.3 copy-start.2
